TPU v7x, 128 devices: a whole 4x4x4 slice. The times are simulated.
128 devices in a mesh: row: 8 (over z, y_lo), col: 16 (over y_hi, x, core).
Axes of the slice: x: 4, y: 4 (y_hi: 2, y_lo: 2; y = y_hi * 2 + y_lo), z: 4, core: 2. Of those that a mesh axis runs over, the one named last changes fastest.
Arguments:
- joined_weight: bfloat16 [16, 2880, 5760], P('row', 'col'), may hold values from -0.109375 to 0.109375
- tile_perm: int32 [144], replicated, may hold values from 0 to 143, each once
- down_weight: bfloat16 [16, 2880, 2880], P('row', 'col'), may hold values from -0.109375 to 0.109375
- tokens: bfloat16 [1024, 2880], P(('row', 'col')), may hold values from -6 to 6
- expert_ids: int32 [1024, 4], replicated, may hold values from 0 to 15, all different within a row; in each aligned block of 1024 rows (0 to 1023, 1024 to 2047, ...) at most 512 rows name the same one
- route_scores: float32 [1024, 4], replicated, may hold values from 0.1 to 1
Outputs:
- gate_weight: bfloat16 [16, 2880, 2880], P('row', None, 'col')
- up_weight: bfloat16 [16, 2880, 2880], P('row', None, 'col')
- mixed: bfloat16 [1024, 2880], P(('row', 'col'))
Inputs may be any that keep to these rules, and one draw needn't show every extreme that they name: `expert_ids`: every expert is chosen by at most 512 tokens, a bound that some block reaches.
All inputs are finite; a program needn't handle non-finite values.
Results may differ from a plain program's by a relative error of at most 0.0049.
Values may be sent and summed in bfloat16 or wider, within the bound.
No kernel may reach another device: no remote copies, remote signals or barrier semaphores. Data moves between devices by JAX's collectives and lax.ppermute only.
A program may use at most 128 MiB of HBM per device.

v0:
```python
import jax
import jax.numpy as jnp
from jax import lax
from jax.sharding import PartitionSpec as P


def body(joined_weight, tile_perm, down_weight, tokens, expert_ids, route_scores):
    n_col = lax.axis_size("col")
    local = joined_weight.shape[0]
    width = joined_weight.shape[2]
    ff_local = width // 2 // n_col
    tiles = tile_perm.shape[0]
    tile_cols = width // tiles
    places = jnp.arange(tiles, dtype=jnp.int32)
    inverse = jnp.sum(places[:, None] * (tile_perm[:, None] == places[None, :]), axis=0)
    order = jnp.arange(width, dtype=jnp.int32)
    lookup = (order // tile_cols)[:, None] == places[None, :]
    stored = jnp.sum(lookup * inverse[None, :], axis=1) * tile_cols + order % tile_cols
    packed = jnp.take(joined_weight, stored, axis=2)
    everything = lax.all_gather(tokens, ("row", "col"), axis=0, tiled=True)
    expert_global = lax.axis_index("row") * local + jnp.arange(local, dtype=jnp.int32)
    weights = route_scores / jnp.sum(route_scores, axis=1, keepdims=True)
    share = jnp.sum(
        weights[:, :, None] * (expert_ids[:, :, None] == expert_global[None, None, :]), axis=1
    )
    weights_in = lax.all_to_all(packed, "col", split_axis=2, concat_axis=1, tiled=True)
    count = weights_in.shape[0]
    paired = weights_in.reshape(count, weights_in.shape[1], ff_local, 2)
    gate_part = paired[:, :, :, 0]
    up_part = paired[:, :, :, 1]
    pre_gate = jnp.einsum("td,ndf->ntf", everything, gate_part, preferred_element_type=jnp.float32)
    pre_up = jnp.einsum("td,ndf->ntf", everything, up_part, preferred_element_type=jnp.float32)
    gate_out, up_out = (gate_part, up_part)
    pre_gate, pre_up = (pre_gate, pre_up)
    active = share.T[:, :, None] * (pre_up + 1.0) * pre_gate * jax.nn.sigmoid(1.702 * pre_gate)
    active = active.astype(jnp.bfloat16)
    total = lax.psum_scatter(
        jnp.einsum("ntf,nfd->td", active, down_weight, preferred_element_type=jnp.float32),
        ("row", "col"),
        scatter_dimension=0,
        tiled=True,
    )
    return (gate_out, up_out, total.astype(jnp.bfloat16))


def solution(mesh):
    placed = (P("row", "col", None), P(), P("row", "col", None), P(("row", "col"), None), P(), P())
    return jax.shard_map(
        body,
        mesh=mesh,
        in_specs=placed,
        out_specs=(P("row", None, "col"), P("row", None, "col"), P(("row", "col"), None)),
        check_vma=False,
    )
```

profile of v0, /device:TPU:0, one launch (start us, length us, event | category | flops | bytes accessed | tf_op | source)
XLA Modules:
  0.0 425.9 jit_solution(15690301397363890240)
XLA Ops:
  7.2 0.0 all-gather.2.cloned.1.call-start
  7.2 0.7 all-gather.2.cloned.1.call-update
  7.9 19.8 %copy.38 = bf16[2,180,5760]{1,0,2:T(2,128)(2,1)} copy(bf16[2,180,5760]{2,0,1:T(2,128)(2,1)} %param.6) | data formatting | bytes 8294400 | tf_op args[0]
  27.7 0.1 select_reduce_fusion.1
  27.8 0.6 select_reduce_fusion
  28.4 0.1 fusion.22
  28.6 25.1 %gather_fusion = bf16[5760,2,180]{2,1,0:T(2,128)(2,1)} fusion(bf16[2,180,5760]{1,0,2:T(2,128)(2,1)} %copy.38, s32[6144]{0:T(1024)S(1)} %pad_clamp_fusion), kind=kCustom, calls=%fused_computation | custom fusion | bytes 8317440 | tf_op jit(solution)/shard_map/jit(_take)/gather | solution.py:19
  53.7 22.9 %fusion.4 = bf16[2,180,5760]{1,0,2:T(2,128)(2,1)} fusion(bf16[5760,2,180]{2,1,0:T(2,128)(2,1)} %gather_fusion, pred[5760]{0:T(1024)(128)(4,1)S(1)} %compare_and_fusion), kind=kLoop, calls=%fused_computation.8 | loop fusion | flops 2073600 | bytes 8300160 | tf_op jit(solution)/shard_map/jit(_take)/select_n | solution.py:19
  76.6 7.4 %all-to-all-start = ((bf16[2,180,5760]{1,0,2:T(2,128)(2,1)}), bf16[2,180,5760]{1,0,2:T(2,128)(2,1)}, u32[]{:S(2)}, u32[]{:S(2)}) async-start(bf16[2,180,5760]{1,0,2:T(2,128)(2,1)} %fusion.4), calls=%async_computation | async-start | bytes 11796480 | tf_op jit(solution)/shard_map/all_to_all | solution.py:26
  84.1 0.1 select_reduce_fusion.2
  84.2 80.8 %all-to-all-done = bf16[2,180,5760]{1,0,2:T(2,128)(2,1)} async-done(((bf16[2,180,5760]{1,0,2:T(2,128)(2,1)}), bf16[2,180,5760]{1,0,2:T(2,128)(2,1)}, u32[]{:S(2)}, u32[]{:S(2)}) %all-to-all-start) | async-done | bytes 4147232 | tf_op jit(solution)/shard_map/all_to_all | solution.py:26
  165.0 7.3 %copy.51 = bf16[2,180,16,360]{1,2,3,0:T(8,128)(2,1)} copy(bf16[2,180,16,360]{1,0,3,2:T(2,128)(2,1)} %bitcast.1) | data formatting | bytes 8294400 | tf_op jit(solution)/shard_map/all_to_all | solution.py:26
  172.3 18.4 %reshape.79 = bf16[2,2880,180,2]{1,3,2,0:T(2,128)(2,1)} reshape(bf16[2,16,180,360]{2,1,3,0:T(8,128)(2,1)} %bitcast.36) | data formatting | bytes 8294400 | tf_op jit(solution)/shard_map/reshape | solution.py:28
  190.7 9.2 %fusion.25 = (bf16[2,2880,180,1]{1,3,2,0:T(2,128)(2,1)S(1)}, bf16[2,2880,180,1]{1,3,2,0:T(2,128)(2,1)S(1)}) fusion(bf16[2,2880,180,2]{1,3,2,0:T(2,128)(2,1)} %reshape.79), kind=kLoop, calls=%fused_computation.44 | loop fusion | bytes 8294400 | tf_op jit(solution)/shard_map/slice | solution.py:30
  199.9 0.2 copy.52
  200.2 3.0 copy.42
  203.1 0.2 copy.53
  203.4 1.3 copy-done.2
  204.7 3.0 copy.43
  207.7 69.3 %all-gather.2.cloned.1.call-done = bf16[1024,2880]{1,0:T(8,128)(2,1)} async-done(((bf16[8,2880]{1,0:T(8,128)(2,1)}), bf16[1024,2880]{1,0:T(8,128)(2,1)}) %all-gather.2.cloned.1.call-update) | async-done | bytes 5898256 | tf_op jit(solution)/shard_map/all_gather | solution.py:20
  277.0 7.1 %fusion = f32[2,180,1024]{2,1,0:T(8,128)} fusion(bf16[2,2880,180]{1,2,0:T(8,128)(2,1)} %bitcast.38, bf16[1024,2880]{1,0:T(8,128)(2,1)} %all-gather.2.cloned.1.call-done), kind=kOutput, calls=%fused_computation.3 | convolution fusion | flops 2123366400 | bytes 9446400 | tf_op jit(solution)/shard_map/td,ndf->ntf/dot_general | solution.py:31
  284.0 14.3 %convolution_bitcast_fusion = f32[1024,2880]{1,0:T(8,128)} fusion(bf16[2,180,2880]{2,0,1:T(2,128)(2,1)S(1)} %copy-done, f32[2,180,1024]{2,1,0:T(8,128)} %fusion, bf16[2,2880,180]{1,2,0:T(8,128)(2,1)} %bitcast.40, bf16[1024,2880]{1,0:T(8,128)(2,1)} %all-gather.2.cloned.1.call-done, f32[2,1024]{1,0:T(2,128)S(1)} %bitcast.41), kind=kOutput, calls=%fused_computation.2 | convolution fusion | flops 4250050560 | bytes 23324672 | tf_op jit(solution)/shard_map/ntf,nfd->td/dot_general | solution.py:38
  298.4 119.3 %all-reduce.2 = bf16[1024,2880]{1,0:T(8,128)(2,1)} all-reduce(f32[1024,2880]{1,0:T(8,128)} %convolution_bitcast_fusion), channel_id=2, replica_groups=mesh['row'=8,'col'=16] {'row','col'}, use_global_device_ids=true, to_apply=%region_4.5.clone | all-reduce | flops 2949120 | bytes 17694720
  417.6 1.4 dynamic-slice_convert_fusion
  (18 shorter events, 0.1 us)
Async XLA Ops:
  7.2 276.9 %copy-start = (bf16[2,180,2880]{2,0,1:T(2,128)(2,1)S(1)}, bf16[2,180,2880]{2,0,1:T(2,128)(2,1)}, u32[]{:S(2)}) copy-start(bf16[2,180,2880]{2,0,1:T(2,128)(2,1)} %param.8) | copy-start | bytes 6220804
  7.2 269.8 %all-gather.2.cloned.1.call-start = ((), (), s32[]{:S(2)}) async-start(), calls=%async_computation.1 | async-start | bytes 6076416 | tf_op jit(solution)/shard_map/all_gather | solution.py:20
  7.9 19.8 %copy-start.5 = (s32[144]{0:T(256)S(1)}, s32[144]{0:T(256)}, u32[]{:S(2)}) copy-start(s32[144]{0:T(256)} %param.7) | copy-start | bytes 1732
  76.6 7.4 %copy-start.3 = (f32[1024,4]{0,1:T(4,128)S(1)}, f32[1024,4]{0,1:T(4,128)}, u32[]{:S(2)}) copy-start(f32[1024,4]{0,1:T(4,128)} %param.11) | copy-start | bytes 49156
  76.6 7.5 %copy-start.4 = (s32[1024,4]{0,1:T(4,128)S(1)}, s32[1024,4]{0,1:T(4,128)}, u32[]{:S(2)}) copy-start(s32[1024,4]{0,1:T(4,128)} %param.10) | copy-start | bytes 49156
  76.6 88.3 %all-to-all-start = ((bf16[2,180,5760]{1,0,2:T(2,128)(2,1)}), bf16[2,180,5760]{1,0,2:T(2,128)(2,1)}, u32[]{:S(2)}, u32[]{:S(2)}) async-start(bf16[2,180,5760]{1,0,2:T(2,128)(2,1)} %fusion.4), calls=%async_computation | async-start | bytes 11796480 | tf_op jit(solution)/shard_map/all_to_all | solution.py:26
  200.2 3.2 copy-start.1
  203.4 1.3 copy-start.2
Sparse Core Ops, SparseCore 0:
  9.7 267.2 all-gather.1
where the time goes:
time: 427 us; the launch traced here: 426 us
  waiting for transfers between devices  151 us (35%)
  blocking collectives  119 us (28%)
  local copies, waits for them, and re-layouts  89 us (21%)
  other arithmetic  23.9 us (6%)
  matrix products  21.4 us (5%)
  between operations  14.2 us (3%)
  starting transfers between devices  7.42 us (2%)
    unnamed x1, blocking collectives  119 us
    all_to_all x1, waiting for transfers between devices, body(): lax.all_to_all(packed, 'col', split_axis=2, concat_axis=1, tiled=True)  80.8 us
    all_gather x1, waiting for transfers between devices, body(): everything = lax.all_gather(tokens, ('row', 'col'), axis=0, tiled=True)  69.3 us
    unnamed x17, local copies, waits for them, and re-layouts  27.5 us
    gather x1, local copies, waits for them, and re-layouts, body(): packed = jnp.take(joined_weight, stored, axis=2)  25.1 us
    select_n x2, other arithmetic, body(): packed = jnp.take(joined_weight, stored, axis=2)  23.1 us
    reshape x1, local copies, waits for them, and re-layouts, body(): paired = weights_in.reshape(count, weights_in.shape[1], ff_local, 2)  18.4 us
    dot_general x1, matrix products, body(): jnp.einsum('ntf,nfd->td', active, down_weight, preferred_element_type=jnp...  14.3 us
  transfers between devices with their start and end apart: 2, of which 2 were waited for; matrix products, arithmetic and copies ran while one was open for 26% of the time, Pallas kernels for 0%

commit v1 on v0

--- a/solution.py
+++ b/solution.py
@@ -17,7 +17,10 @@
     lookup = (order // tile_cols)[:, None] == places[None, :]
     stored = jnp.sum(lookup * inverse[None, :], axis=1) * tile_cols + order % tile_cols
     packed = jnp.take(joined_weight, stored, axis=2)
-    everything = lax.all_gather(tokens, ("row", "col"), axis=0, tiled=True)
+    everything = jnp.concatenate(
+        lax.all_to_all(jnp.stack([tokens] * lax.axis_size(("row", "col"))), ("row", "col"), 0, 0),
+        axis=0,
+    )
     expert_global = lax.axis_index("row") * local + jnp.arange(local, dtype=jnp.int32)
     weights = route_scores / jnp.sum(route_scores, axis=1, keepdims=True)
     share = jnp.sum(

time: 427 us -> 372 us (0.87)
  waiting for transfers between devices: 151 us -> 29 us
  blocking collectives: 119 us -> 196 us
  between operations: 14.2 us -> 0.82 us
    all_to_all x0 -> x1, blocking collectives: none -> 76.8 us  [body(): lax.all_to_all(packed, 'col', split_axis=2, concat_axis=1, tiled=True)]
    all_gather x1 -> x0, waiting for transfers between devices: 69.3 us -> none  [body(): everything = lax.all_gather(tokens, ('row', 'col'), axis=0, tiled=True)]
    all_to_all x1, waiting for transfers between devices: 80.8 us -> 29 us  [body(): lax.all_to_all(jnp.stack([tokens] * lax.axis_size(('row', 'col'))), ('row...]
  transfers between devices with their start and end apart: 2 -> 1, of which waited for: 2 -> 1; matrix products, arithmetic and copies ran while one was open for 26% -> 11% of each run, Pallas kernels for 0% -> 0%
where the time goes in v1:
time: 372 us; the launch traced here: 370 us
  blocking collectives  196 us (53%)
  local copies, waits for them, and re-layouts  92.1 us (25%)
  waiting for transfers between devices  29 us (8%)
  other arithmetic  24.2 us (7%)
  matrix products  21.1 us (6%)
  starting transfers between devices  7.45 us (2%)
    unnamed x1, blocking collectives  119 us
    all_to_all x1, blocking collectives, body(): lax.all_to_all(packed, 'col', split_axis=2, concat_axis=1, tiled=True)  76.8 us
    all_to_all x1, waiting for transfers between devices, body(): lax.all_to_all(jnp.stack([tokens] * lax.axis_size(('row', 'col'))), ('row...  29 us
    unnamed x17, local copies, waits for them, and re-layouts  27.5 us
    gather x1, local copies, waits for them, and re-layouts, body(): packed = jnp.take(joined_weight, stored, axis=2)  25.1 us
    select_n x2, other arithmetic, body(): packed = jnp.take(joined_weight, stored, axis=2)  22.5 us
    reshape x1, local copies, waits for them, and re-layouts, body(): paired = weights_in.reshape(count, weights_in.shape[1], ff_local, 2)  18.4 us
    dot_general x1, matrix products, body(): jnp.einsum('ntf,nfd->td', active, down_weight, preferred_element_type=jnp...  14 us
  transfers between devices with their start and end apart: 1, of which 1 were waited for; matrix products, arithmetic and copies ran while one was open for 11% of the time, Pallas kernels for 0%

profile of v1, /device:TPU:0, one launch (start us, length us, event | category | flops | bytes accessed | tf_op | source)
XLA Modules:
  0.0 370.5 jit_solution(16177325848410322226)
XLA Ops:
  0.6 0.0 copy-start
  0.7 0.9 select_reduce_fusion.1
  1.6 0.6 select_reduce_fusion
  2.2 19.8 %copy.44 = bf16[2,180,5760]{1,0,2:T(2,128)(2,1)} copy(bf16[2,180,5760]{2,0,1:T(2,128)(2,1)} %param.6) | data formatting | bytes 8294400 | tf_op args[0]
  22.0 0.1 fusion.22
  22.2 25.1 %gather_fusion = bf16[5760,2,180]{2,1,0:T(2,128)(2,1)} fusion(bf16[2,180,5760]{1,0,2:T(2,128)(2,1)} %copy.44, s32[6144]{0:T(1024)S(1)} %pad_clamp_fusion), kind=kCustom, calls=%fused_computation | custom fusion | bytes 8317440 | tf_op jit(solution)/shard_map/jit(_take)/gather | solution.py:19
  47.2 22.3 %fusion.4 = bf16[2,180,5760]{1,0,2:T(2,128)(2,1)S(1)} fusion(bf16[5760,2,180]{2,1,0:T(2,128)(2,1)} %gather_fusion, pred[5760]{0:T(1024)(128)(4,1)S(1)} %compare_and_fusion), kind=kLoop, calls=%fused_computation.8 | loop fusion | flops 2073600 | bytes 8300160 | tf_op jit(solution)/shard_map/jit(_take)/select_n | solution.py:19
  69.6 76.8 %all_to_all.20 = bf16[2,180,5760]{1,0,2:T(2,128)(2,1)} all-to-all(bf16[2,180,5760]{1,0,2:T(2,128)(2,1)S(1)} %fusion.4), channel_id=1, replica_groups=mesh['row'=8,'col'=16] {'col'}, dimensions={2} | all-to-all | bytes 8294400 | tf_op jit(solution)/shard_map/all_to_all | solution.py:29
  146.4 3.0 stack.2
  149.4 7.5 %all-to-all-start.1 = ((bf16[128,8,2880]{2,1,0:T(8,128)(2,1)}), bf16[128,8,2880]{2,1,0:T(8,128)(2,1)}, u32[]{:S(2)}, u32[]{:S(2)}) async-start(bf16[128,8,2880]{2,1,0:T(8,128)(2,1)} %stack.2), calls=%async_computation.1 | async-start | bytes 12058624 | tf_op jit(solution)/shard_map/all_to_all | solution.py:21
  156.9 0.1 select_reduce_fusion.2
  157.0 7.3 %copy.63 = bf16[2,180,16,360]{1,2,3,0:T(8,128)(2,1)} copy(bf16[2,180,16,360]{1,0,3,2:T(2,128)(2,1)} %bitcast.39) | data formatting | bytes 8294400 | tf_op jit(solution)/shard_map/all_to_all | solution.py:29
  164.4 18.4 %reshape.84 = bf16[2,2880,180,2]{1,3,2,0:T(2,128)(2,1)} reshape(bf16[2,16,180,360]{2,1,3,0:T(8,128)(2,1)} %bitcast.40) | data formatting | bytes 8294400 | tf_op jit(solution)/shard_map/reshape | solution.py:31
  182.8 9.4 %fusion.25 = (bf16[2,2880,180,1]{1,3,2,0:T(2,128)(2,1)S(1)}, bf16[2,2880,180,1]{1,3,2,0:T(2,128)(2,1)S(1)}) fusion(bf16[2,2880,180,2]{1,3,2,0:T(2,128)(2,1)} %reshape.84), kind=kLoop, calls=%fused_computation.44 | loop fusion | bytes 8294400 | tf_op jit(solution)/shard_map/slice | solution.py:33
  192.2 0.2 copy.64
  192.4 3.0 copy.50
  195.4 0.2 copy.65
  195.7 1.3 copy-done.2
  197.0 3.0 copy.51
  199.9 29.0 %all-to-all-done.1 = bf16[128,8,2880]{2,1,0:T(8,128)(2,1)} async-done(((bf16[128,8,2880]{2,1,0:T(8,128)(2,1)}), bf16[128,8,2880]{2,1,0:T(8,128)(2,1)}, u32[]{:S(2)}, u32[]{:S(2)}) %all-to-all-start.1) | async-done | bytes 5898272 | tf_op jit(solution)/shard_map/all_to_all | solution.py:21
  228.9 7.0 %fusion = f32[2,180,1024]{2,1,0:T(8,128)} fusion(bf16[2,2880,180]{1,2,0:T(8,128)(2,1)} %bitcast.42, bf16[128,8,2880]{2,1,0:T(8,128)(2,1)} %all-to-all-done.1), kind=kOutput, calls=%fused_computation.3 | convolution fusion | flops 2123366400 | bytes 9446400 | tf_op jit(solution)/shard_map/td,ndf->ntf/dot_general | solution.py:34
  235.9 14.0 %convolution_bitcast_fusion = f32[1024,2880]{1,0:T(8,128)} fusion(bf16[2,180,2880]{2,0,1:T(2,128)(2,1)S(1)} %copy-done, f32[2,180,1024]{2,1,0:T(8,128)} %fusion, bf16[2,2880,180]{1,2,0:T(8,128)(2,1)} %bitcast.44, bf16[128,8,2880]{2,1,0:T(8,128)(2,1)} %all-to-all-done.1, f32[2,1024]{1,0:T(2,128)S(1)} %bitcast.45), kind=kOutput, calls=%fused_computation.2 | convolution fusion | flops 4250050560 | bytes 23324672 | tf_op jit(solution)/shard_map/ntf,nfd->td/dot_general | solution.py:41
  250.0 119.1 %all-reduce.2 = bf16[1024,2880]{1,0:T(8,128)(2,1)} all-reduce(f32[1024,2880]{1,0:T(8,128)} %convolution_bitcast_fusion), channel_id=2, replica_groups=mesh['row'=8,'col'=16] {'row','col'}, use_global_device_ids=true, to_apply=%region_4.5.clone | all-reduce | flops 2949120 | bytes 17694720
  369.1 1.4 dynamic-slice_convert_fusion
  (17 shorter events, 0.1 us)
Async XLA Ops:
  0.6 235.3 %copy-start = (bf16[2,180,2880]{2,0,1:T(2,128)(2,1)S(1)}, bf16[2,180,2880]{2,0,1:T(2,128)(2,1)}, u32[]{:S(2)}) copy-start(bf16[2,180,2880]{2,0,1:T(2,128)(2,1)} %param.8) | copy-start | bytes 6220804
  69.5 76.8 %copy-start.4 = (bf16[8,2880]{1,0:T(8,128)(2,1)S(1)}, bf16[8,2880]{1,0:T(8,128)(2,1)}, u32[]{:S(2)}) copy-start(bf16[8,2880]{1,0:T(8,128)(2,1)} %param.9) | copy-start | bytes 138244
  149.4 7.5 %copy-start.3 = (f32[1024,4]{0,1:T(4,128)S(1)}, f32[1024,4]{0,1:T(4,128)}, u32[]{:S(2)}) copy-start(f32[1024,4]{0,1:T(4,128)} %param.11) | copy-start | bytes 49156
  149.4 7.5 %copy-start.5 = (s32[1024,4]{0,1:T(4,128)S(1)}, s32[1024,4]{0,1:T(4,128)}, u32[]{:S(2)}) copy-start(s32[1024,4]{0,1:T(4,128)} %param.10) | copy-start | bytes 49156
  149.4 79.5 %all-to-all-start.1 = ((bf16[128,8,2880]{2,1,0:T(8,128)(2,1)}), bf16[128,8,2880]{2,1,0:T(8,128)(2,1)}, u32[]{:S(2)}, u32[]{:S(2)}) async-start(bf16[128,8,2880]{2,1,0:T(8,128)(2,1)} %stack.2), calls=%async_computation.1 | async-start | bytes 12058624 | tf_op jit(solution)/shard_map/all_to_all | solution.py:21
  192.4 3.2 copy-start.1
  195.6 1.3 copy-start.2
